TPU v7x, 32 devices: a whole 2x2x4 slice. The times are simulated.
32 devices in a mesh: group: 2 (over x), grid: 8 (over z, y), var: 2 (over core).
Axes of the slice: x: 2, y: 2, z: 4, core: 2. Of those that a mesh axis runs over, the one named last changes fastest.
Arguments:
- tokens: bfloat16 [96, 96, 3, 512], P('group', 'grid'), parts along dimension 0, may hold values from -6 to 6
- key_mask: int32 [96, 96], P('group', 'grid'), parts along dimension 0, may hold values 0 or 1
- w_qkv: bfloat16 [3, 512, 512], P(None, None, 'var'), may hold values from -16 to 16
- w_proj: bfloat16 [512, 512], P('var'), may hold values from -0.25 to 0.25
- w_up: bfloat16 [512, 2048], P(None, 'var'), may hold values from -0.25 to 0.25
- w_down: bfloat16 [2048, 512], P('var'), may hold values from -0.125 to 0.125
- level_query: bfloat16 [13, 512], replicated, may hold values from -1200 to 1200
- w_dec_q: bfloat16 [512, 512], P(None, 'var'), may hold values from -0.25 to 0.25
- w_dec_kv: bfloat16 [2, 512, 512], P(None, None, 'var'), may hold values from -0.25 to 0.25
- w_dec_o: bfloat16 [512, 512], P('var'), may hold values from -0.25 to 0.25
- decode_matrix: float32 [512, 64], replicated, may hold values from -0.25 to 0.25
Outputs:
- estimated_maps: float32 [4, 26, 192, 384], P('var', 'group', 'grid'), parts along dimension 1
There are 2 independent parts, one for each index of `group`. A program takes and returns all parts, laid end to end along the dimension named above; an argument that names none is the same for every part. Nothing has to cross between parts.
All inputs are finite; a program needn't handle non-finite values. No bound on the sum of `key_mask` on one device may be relied on, other than what follows from the above.
Results may differ from a plain program's by a relative error of at most 0.025.
Values may be sent and summed in bfloat16 or wider, within the bound.
A program may use at most 128 MiB of HBM per device.

v0:
```python
import functools

import jax
import jax.numpy as jnp
import numpy as np
from jax import lax
from jax.experimental import pallas as pl
from jax.experimental.pallas import tpu as pltpu
from jax.sharding import PartitionSpec as P

HD = 64
TARGET_QUANTITY = 4
SQUARE_SPAN = 4
WIN_LAT = 6
EPSILON = 1e-05
BLOCK = 128
KEYS = 256
CHUNK = 256
LEVEL_SLOTS = 16
MESH = pl.DeviceIdType.MESH
NT = (((1,), (1,)), ((), ()))
F32 = jnp.float32
BF16 = jnp.bfloat16


def layer_norm(values):
    center = values - jnp.mean(values, axis=-1, keepdims=True)
    spread = jnp.mean(center * center, axis=-1, keepdims=True)
    return center * lax.rsqrt(spread + EPSILON)


class Geometry:
    def __init__(self, tokens, w_proj, level_query, decode_matrix, cores, bands):
        self.rows, self.cols, self.levels, self.features = tokens.shape
        self.cores, self.bands = cores, bands
        self.half_cols = self.cols // 2
        self.row_count = self.rows // cores
        self.windows = self.row_count // WIN_LAT
        self.taken = 8 * (-(-(self.row_count + WIN_LAT // 2) // 8))
        self.half_patches = WIN_LAT * self.half_cols
        self.half = 16 * (-(-(self.levels * self.half_patches) // 16))
        self.tokens = 2 * self.half
        self.patches = 2 * self.half_patches
        self.width = w_proj.shape[0]
        self.heads = self.width // HD
        self.isobars = level_query.shape[0]
        self.slots = self.isobars + self.isobars % 2
        self.pixels = decode_matrix.shape[1]
        self.scatter = bands * WIN_LAT == self.rows and (bands * self.cols * SQUARE_SPAN) % BLOCK == 0

    def place(self, half, level, r, c):
        return half * self.half + level * self.half_patches + r * self.half_cols + c

    def each(self):
        for half in range(2):
            for level in range(self.levels):
                for r in range(WIN_LAT):
                    for c in range(self.half_cols):
                        yield half, level, r, c

    def gather_table(self):
        table = np.zeros((self.windows, self.half, self.half_cols * self.levels * self.taken), np.float32)
        for w in range(self.windows):
            for half, level, r, c in self.each():
                if half == 0:
                    source = (c * self.levels + level) * self.taken + WIN_LAT * w + WIN_LAT // 2 + r
                    table[w, self.place(0, level, r, c), source] = 1.0
        return table.reshape(self.windows * self.half, -1)

    def order_table(self):
        table = np.zeros((KEYS, self.tokens), np.float32)
        for half, level, r, c in self.each():
            patch = r * self.cols + half * self.half_cols + c
            table[level * self.patches + patch, self.place(half, level, r, c)] = 1.0
        return table

    def position_table(self):
        table = np.full((8, KEYS), -1, np.int32)
        table[0] = 0
        for half, level, r, c in self.each():
            at = self.place(half, level, r, c)
            table[0, at] = r
            table[1 + half, at] = c + (self.half_cols if half == 0 else 0)
        return table

    def pixel_table(self):
        table = np.zeros((self.pixels, self.pixels), np.float32)
        own = TARGET_QUANTITY // self.cores
        for v in range(TARGET_QUANTITY):
            for a in range(SQUARE_SPAN):
                for b in range(SQUARE_SPAN):
                    target = ((v // own * SQUARE_SPAN + b) * own + v % own) * SQUARE_SPAN + a
                    table[target, (v * SQUARE_SPAN + a) * SQUARE_SPAN + b] = 1.0
        return table

    def pick_table(self):
        half_lat = WIN_LAT // 2
        run = self.cols * SQUARE_SPAN
        picks = np.zeros((SQUARE_SPAN, BLOCK, 3 * BLOCK), np.float32)
        for ih in range(2):
            for q in range(half_lat * run):
                r, rest = divmod(q, run)
                column, b = divmod(rest, SQUARE_SPAN)
                source = (half_lat * ih + r) * self.cols + column
                target = ih * BLOCK + q if q < BLOCK else 2 * BLOCK + ih * (BLOCK // 2) + q - BLOCK
                picks[b, source, target] = 1.0
        return picks


def fold_decoder(lq, wq, wkv_ref, wo, dm, perm, out_ref):
    width = wq.shape[1]
    heads = width // HD
    dquery = jnp.dot(lq, wq, preferred_element_type=F32) * HD ** (-0.5)
    d_hi = dquery.astype(BF16)
    d_lo = (dquery - d_hi.astype(F32)).astype(BF16)
    count = LEVEL_SLOTS * heads
    row = lax.broadcasted_iota(jnp.int32, (count, dquery.shape[0]), 0)
    slot = lax.broadcasted_iota(jnp.int32, (count, dquery.shape[0]), 1)
    spread = (row // heads == slot).astype(F32).astype(BF16)
    row = lax.broadcasted_iota(jnp.int32, (count, width), 0)
    mine = row % heads == lax.broadcasted_iota(jnp.int32, (count, width), 1) // HD
    q_hi = jnp.dot(spread, d_hi, preferred_element_type=F32)
    q_hi = jnp.where(mine, q_hi, 0.0).astype(BF16)
    q_lo = jnp.dot(spread, d_lo, preferred_element_type=F32)
    q_lo = jnp.where(mine, q_lo, 0.0).astype(BF16)
    wk = wkv_ref[0]
    g = lax.dot_general(q_hi, wk, NT, preferred_element_type=F32)
    g = g + lax.dot_general(q_lo, wk, NT, preferred_element_type=F32)
    g_hi = g.astype(BF16)
    out_ref[0, 0:count, :] = g_hi
    out_ref[0, count : 2 * count, :] = (g - g_hi.astype(F32)).astype(BF16)
    dm_hi = dm.astype(BF16)
    dm_lo = (dm - dm_hi.astype(F32)).astype(BF16)
    dm_hi = jnp.dot(perm, dm_hi, preferred_element_type=F32).astype(BF16)
    dm_lo = jnp.dot(perm, dm_lo, preferred_element_type=F32).astype(BF16)
    m_t = lax.dot_general(dm_hi, wo, NT, preferred_element_type=F32)
    m_t = m_t + lax.dot_general(dm_lo, wo, NT, preferred_element_type=F32)
    pixels = m_t.shape[0]
    stacked = jnp.concatenate([m_t] * heads, axis=0)
    row_head = lax.broadcasted_iota(jnp.int32, stacked.shape, 0) // pixels
    lane_head = lax.broadcasted_iota(jnp.int32, stacked.shape, 1) // HD
    stacked = jnp.where(row_head == lane_head, stacked, 0.0)
    s_hi = stacked.astype(BF16)
    s_lo = (stacked - s_hi.astype(F32)).astype(BF16)
    wv = wkv_ref[1]
    n_t = lax.dot_general(s_hi, wv, NT, preferred_element_type=F32)
    n_t = n_t + lax.dot_general(s_lo, wv, NT, preferred_element_type=F32)
    out_ref[0, 2 * count :, :] = n_t.astype(BF16)


def main_kernel(
    geo,
    tok_ref,
    mask_ref,
    wqkv_ref,
    wproj_ref,
    wup_ref,
    wdown_ref,
    lq_ref,
    wq_ref,
    wkv_ref,
    wo_ref,
    dm_ref,
    gather_ref,
    order_ref,
    position_ref,
    perm_ref,
    pick_ref,
    out_ref,
    raw,
    marks,
    qkv,
    proj,
    up,
    down,
    lq,
    wq,
    wkv,
    wo,
    dm,
    gather,
    order,
    position,
    perm,
    pick,
    fold,
    first,
    own,
    halo,
    differs,
    hid,
    dw,
    du,
    base_pix,
    pix,
    pieces,
    checked,
    load_sem,
    weight_send,
    weight_recv,
    halo_send,
    halo_recv,
    piece_send,
    piece_recv,
):
    group, grid, var = (lax.axis_index(name) for name in ("group", "grid", "var"))
    bands, cores, windows, half = geo.bands, geo.cores, geo.windows, geo.half
    features, levels, width, heads = geo.features, geo.levels, geo.width, geo.heads
    sibling = (group, grid, lax.rem(var + 1, cores))
    west = (group, lax.rem(grid + bands - 1, bands), var)
    east = (group, lax.rem(grid + 1, bands), var)
    barrier = pltpu.get_barrier_semaphore()
    if geo.scatter:
        peers = bands * cores
        me = grid * cores + var

        @pl.loop(1, peers)
        def _(step):
            peer = lax.rem(me + step, peers)
            pl.semaphore_signal(
                barrier, inc=1, device_id=(group, peer // cores, lax.rem(peer, cores)), device_id_type=MESH
            )

        greeted = peers - 1
    else:
        for peer in (sibling, west, east):
            pl.semaphore_signal(barrier, inc=1, device_id=peer, device_id_type=MESH)
        greeted = 3

    loads = []

    def load(source, target):
        copy = pltpu.make_async_copy(source, target, load_sem.at[len(loads)])
        copy.start()
        loads.append(copy)
        return copy

    tiles = geo.rows // 8
    first_tile = var * (geo.row_count // 8)
    slabs = []
    for s in range(geo.taken // 8):
        tile = lax.rem(first_tile + s, tiles)
        slabs.append(
            load(tok_ref.at[:, :, pl.ds(pl.multiple_of(tile * 8, 8), 8), :], raw.at[:, :, 8 * s : 8 * s + 8, :])
        )
    gather_load = load(gather_ref, gather)
    fold_loads = [
        load(a, b)
        for a, b in ((lq_ref, lq), (wq_ref, wq), (wkv_ref, wkv), (wo_ref, wo), (dm_ref, dm), (perm_ref, perm))
    ]
    late_loads = [
        load(a, b)
        for a, b in (
            (mask_ref, marks.at[0]),
            (wqkv_ref, qkv.at[0]),
            (wproj_ref, proj.at[0]),
            (wup_ref, up.at[0]),
            (wdown_ref, down.at[0]),
            (position_ref, position),
            (order_ref, order),
            (pick_ref, pick),
        )
    ]

    for copy in slabs:
        copy.wait()
    gather_load.wait()
    depth = geo.half_cols * levels * geo.taken
    for h, target in ((0, first), (1, own)):
        slab = raw[h * geo.half_cols : (h + 1) * geo.half_cols].reshape(depth, features)
        for c in range(0, features, CHUNK):
            rows = jnp.dot(gather[...], slab[:, c : c + CHUNK], preferred_element_type=F32).astype(BF16)
            target[:, :, c : c + CHUNK] = rows.reshape(windows, half, CHUNK)

    pl.semaphore_wait(barrier, greeted)

    def remote(source, target, send, recv, peer):
        copy = pltpu.make_async_remote_copy(
            src_ref=source, dst_ref=target, send_sem=send, recv_sem=recv, device_id=peer, device_id_type=MESH
        )
        copy.start()
        return copy

    copies = [remote(mask_ref, marks.at[1], weight_send.at[0], weight_recv.at[0], west)]
    halos = []
    for w in range(windows):
        halos.append(remote(first.at[w], halo.at[w], halo_send.at[w], halo_recv.at[w], west))
    for n, (source, target) in enumerate(((wqkv_ref, qkv), (wproj_ref, proj), (wup_ref, up), (wdown_ref, down))):
        copies.append(remote(source, target.at[1], weight_send.at[n + 1], weight_recv.at[n + 1], sibling))

    for copy in fold_loads:
        copy.wait()
    fold_decoder(lq[...], wq[...], wkv, wo[...], dm[...], perm[...], fold)

    tokens = geo.tokens
    q_pos = lax.broadcasted_iota(jnp.int32, (tokens, KEYS), 0)
    k_pos = lax.broadcasted_iota(jnp.int32, (tokens, KEYS), 1)
    diagonal = q_pos == k_pos

    def region_of(pos):
        pos = jnp.where(pos >= half, pos - half, pos)
        for level in range(levels - 1, 0, -1):
            start = geo.half_patches * level
            pos = jnp.where(pos >= start, pos - geo.half_patches, pos) if level == 1 else jnp.where(
                pos >= start, pos - start, pos
            )
        return pos >= geo.half_patches // 2

    differs[...] = jnp.where(region_of(q_pos) != region_of(k_pos), -1e30, 0.0)
    lane_head = lax.broadcasted_iota(jnp.int32, (tokens, width), 1) // HD
    lane_head_keys = lax.broadcasted_iota(jnp.int32, (KEYS, width), 1) // HD

    for copy in late_loads:
        copy.wait()
    copies.append(remote(fold.at[0], fold.at[1], weight_send.at[5], weight_recv.at[5], sibling))
    for copy in copies:
        copy.wait()

    count = heads * LEVEL_SLOTS
    pixels = geo.pixels
    patches = geo.patches
    row_size = pixels // cores // SQUARE_SPAN
    rows = geo.slots * row_size
    half_lat = WIN_LAT // 2
    extra = half_lat * geo.cols * SQUARE_SPAN - BLOCK
    pair = 8 // heads

    def piece_copy(w, ih, core, action):
        band = lax.rem(var * windows + w + ih, bands)
        here = jnp.logical_and(band == grid, core == var)
        source, target = pieces.at[w, ih, core], out_ref.at[grid, ih]

        @pl.when(here)
        def _():
            if action == "start":
                pltpu.make_async_copy(source, target, piece_recv.at[grid, ih]).start()

        @pl.when(jnp.logical_not(here))
        def _():
            if action == "start":
                pltpu.make_async_remote_copy(
                    src_ref=source,
                    dst_ref=target,
                    send_sem=piece_send.at[w, ih, core],
                    recv_sem=piece_recv.at[grid, ih],
                    device_id=(group, band, core),
                    device_id_type=MESH,
                ).start()
            else:
                pltpu.make_async_copy(source, source, piece_send.at[w, ih, core]).wait()

    @pl.loop(0, windows)
    def _(w):
        pltpu.make_async_copy(halo.at[w], halo.at[w], halo_recv.at[w]).wait()
        x = jnp.concatenate([own[w], halo[w]], axis=0).astype(F32)
        n1 = layer_norm(x).astype(BF16)
        target = position[0:1, :] + (var * geo.row_count + WIN_LAT * w + half_lat)
        target = jnp.where(target >= geo.rows, target - geo.rows, target)
        there = lax.broadcasted_iota(jnp.int32, (geo.rows, KEYS), 0) == target
        there = there.astype(F32).astype(BF16)
        opened = jnp.zeros((1, KEYS), F32)
        column = lax.broadcasted_iota(jnp.int32, (geo.cols, KEYS), 0)
        for h in range(2):
            seen = (marks[h] > 0).astype(F32).astype(BF16)
            seen = jnp.dot(seen, there, preferred_element_type=F32)
            seen = jnp.where(column == position[1 + h : 2 + h, :], seen, 0.0)
            opened = opened + jnp.sum(seen, axis=0, keepdims=True)
        allowed = jnp.logical_or(jnp.broadcast_to(opened, diagonal.shape) > 0.5, diagonal)
        cut = jnp.logical_and(var == cores - 1, w == windows - 1)
        bias = jnp.where(allowed, 0.0, -1e30) + differs[...] * jnp.where(cut, 1.0, 0.0)
        attended = jnp.zeros((tokens, features), F32)
        for s in range(cores):
            q = jnp.dot(n1, qkv[s, 0], preferred_element_type=F32).astype(BF16)
            q = q * jnp.asarray(HD ** (-0.5), BF16)
            k = jnp.dot(n1, qkv[s, 1], preferred_element_type=F32).astype(BF16)
            v = jnp.dot(n1, qkv[s, 2], preferred_element_type=F32).astype(BF16)
            tail = jnp.zeros((KEYS - tokens, width), BF16)
            k = jnp.concatenate([k, tail], axis=0)
            v = jnp.concatenate([v, tail], axis=0)
            q_all = jnp.concatenate(
                [jnp.where(lane_head == h, q, jnp.zeros_like(q)) for h in range(heads)], axis=0
            )
            scores = lax.dot_general(q_all, k, NT, preferred_element_type=F32)
            weights = []
            for h in range(heads):
                one = scores[h * tokens : (h + 1) * tokens] + bias
                peak = jnp.max(one, axis=-1, keepdims=True)
                e = jnp.exp(one - peak)
                total = jnp.sum(e, axis=-1, keepdims=True)
                weights.append((e * (1.0 / total)).astype(BF16))
            weights = jnp.concatenate(weights, axis=1)
            v_all = jnp.concatenate(
                [jnp.where(lane_head_keys == h, v, jnp.zeros_like(v)) for h in range(heads)], axis=0
            )
            context = jnp.dot(weights, v_all, preferred_element_type=F32).astype(BF16)
            attended = attended + jnp.dot(context, proj[s], preferred_element_type=F32)
        x_one = x + attended
        n2 = layer_norm(x_one).astype(BF16)
        units = up.shape[2]
        for s in range(cores):
            for c in range(0, units, CHUNK):
                one = jnp.dot(n2, up[s, :, c : c + CHUNK], preferred_element_type=F32)
                one = 0.5 * one * (1.0 + lax.erf(one * 2.0 ** (-0.5)))
                hid[:, s * units + c : s * units + c + CHUNK] = one.astype(BF16)
        latent = x_one + jnp.dot(
            hid[...], down[...].reshape(cores * units, features), preferred_element_type=F32
        )
        n3 = layer_norm(latent.astype(BF16).astype(F32)).astype(BF16)
        n3 = jnp.dot(order[...], n3, preferred_element_type=F32).astype(BF16)

        lane = lax.broadcasted_iota(jnp.int32, (1, BLOCK), 1)

        def by_level(value):
            low, high = value[:, :BLOCK], value[:, BLOCK:]
            found = []
            for level in range(levels):
                start = level * patches
                if start < BLOCK:
                    part = low if start == 0 else pltpu.roll(low, BLOCK - start, 1)
                    if start + patches > BLOCK:
                        part = jnp.where(lane < BLOCK - start, part, pltpu.roll(high, BLOCK - start, 1))
                else:
                    part = pltpu.roll(high, 2 * BLOCK - start, 1) if start > BLOCK else high
                found.append(part)
            return found

        base = jnp.zeros((pixels, BLOCK), F32)
        for s in range(cores):
            g = lax.dot_general(fold[s, 0 : 2 * count, :], n3, NT, preferred_element_type=F32)
            scores = by_level(g[:count] + g[count:])
            peak = functools.reduce(jnp.maximum, scores)
            e = [jnp.exp(one - peak) for one in scores]
            inverse = 1.0 / sum(e)
            for j in range(1, levels):
                dw[j - 1, s * count : (s + 1) * count, :] = e[j] * inverse
            u = by_level(
                lax.dot_general(fold[s, 2 * count :, :], n3, NT, preferred_element_type=F32)
            )
            for h in range(heads):
                base = base + u[0][h * pixels : (h + 1) * pixels]
            for j in range(1, levels):
                du[j - 1, s * heads * pixels : (s + 1) * heads * pixels, :] = u[j] - u[0]
        base_pix[...] = base

        @pl.loop(0, geo.slots // pair)
        def _(at):
            totals = [base_pix[...] for _ in range(pair)]
            for s in range(cores):
                for j in range(levels - 1):
                    start = pl.multiple_of(s * count + at * 8, 8)
                    some = dw[j, pl.ds(start, 8), :]
                    for h in range(heads):
                        top = (s * heads + h) * pixels
                        value = du[j, top : top + pixels, :]
                        for n in range(pair):
                            totals[n] = totals[n] + some[n * heads + h : n * heads + h + 1] * value
            for n in range(pair):
                pix[at * pair + n] = totals[n]

        lane = lax.broadcasted_iota(jnp.int32, (2 * row_size, BLOCK), 1)
        for core in range(cores):
            total = jnp.zeros((rows, 3 * BLOCK), F32)
            for b in range(SQUARE_SPAN):
                top = (core * SQUARE_SPAN + b) * row_size
                part = pix[:, top : top + row_size, :].reshape(rows, BLOCK)
                total = total + jnp.dot(part.astype(BF16), pick[b], preferred_element_type=F32)
            for ih in range(2):
                left = jnp.zeros((2 * row_size, BLOCK), F32)
                for k in range(geo.slots // 2):
                    at = slice(2 * row_size * k, 2 * row_size * (k + 1))
                    moved = pltpu.roll(
                        total[at, 2 * BLOCK :], (extra * k - (BLOCK // 2) * ih) % BLOCK, 1
                    )
                    inside = jnp.logical_and(lane >= extra * k, lane < extra * (k + 1))
                    left = jnp.where(inside, moved, left)
                main = total[:, ih * BLOCK : (ih + 1) * BLOCK]
                pieces[w, ih, core] = jnp.concatenate([main, left], axis=0).astype(BF16)
        if geo.scatter:
            checked[...] = pieces[w].astype(F32).max(axis=(0, 1))
            for ih in range(2):
                for core in range(cores):
                    piece_copy(w, ih, core, "start")

    for copy in halos:
        copy.wait_send()
    if geo.scatter:

        @pl.loop(0, bands)
        def _(s):
            for ih in range(2):
                target = out_ref.at[s, ih]
                pltpu.make_async_copy(target, target, piece_recv.at[s, ih]).wait()

        @pl.loop(0, windows)
        def _(w):
            for ih in range(2):
                for core in range(cores):
                    piece_copy(w, ih, core, "finish")

    else:
        copy = pltpu.make_async_copy(pieces, out_ref, load_sem.at[0])
        copy.start()
        copy.wait()


def forecast(geo, *args):
    tables = (
        jnp.asarray(geo.gather_table(), BF16),
        jnp.asarray(geo.order_table(), BF16),
        jnp.asarray(geo.position_table(), jnp.int32),
        jnp.asarray(geo.pixel_table(), BF16),
        jnp.asarray(geo.pick_table(), BF16),
    )
    features, width, cores, windows = geo.features, geo.width, geo.cores, geo.windows
    units = args[4].shape[1]
    fold_rows = geo.heads * (2 * LEVEL_SLOTS + geo.pixels)
    vmem = pltpu.VMEM
    dma = pltpu.SemaphoreType.DMA
    if geo.scatter:
        out_shape = (geo.bands, 2, BLOCK, BLOCK)
    else:
        out_shape = (windows, 2, cores, BLOCK, BLOCK)
    return pl.pallas_call(
        functools.partial(main_kernel, geo),
        out_shape=jax.ShapeDtypeStruct(out_shape, BF16),
        in_specs=[pl.BlockSpec(memory_space=pltpu.HBM)] * (len(args) + len(tables)),
        out_specs=pl.BlockSpec(memory_space=vmem if geo.scatter else pltpu.HBM),
        scratch_shapes=[
            vmem((geo.cols, geo.levels, geo.taken, features), BF16),
            vmem((2, geo.cols, geo.rows), jnp.int32),
            vmem((cores, 3, features, width), BF16),
            vmem((cores, width, features), BF16),
            vmem((cores, features, units), BF16),
            vmem((cores, units, features), BF16),
            *[vmem(one.shape, one.dtype) for one in args[6:]],
            *[vmem(one.shape, one.dtype) for one in tables],
            vmem((cores, fold_rows, features), BF16),
            vmem((windows, geo.half, features), BF16),
            vmem((windows, geo.half, features), BF16),
            vmem((windows, geo.half, features), BF16),
            vmem((geo.tokens, KEYS), F32),
            vmem((geo.tokens, cores * units), BF16),
            vmem((geo.levels - 1, cores * geo.heads * LEVEL_SLOTS, BLOCK), F32),
            vmem((geo.levels - 1, cores * geo.heads * geo.pixels, BLOCK), F32),
            vmem((geo.pixels, BLOCK), F32),
            vmem((geo.slots, geo.pixels, BLOCK), F32),
            vmem((windows, 2, cores, BLOCK, BLOCK), BF16),
            vmem((BLOCK, BLOCK), F32),
            dma((geo.taken // 8 + 15,)),
            dma((6,)),
            dma((6,)),
            dma((windows,)),
            dma((windows,)),
            dma((windows, 2, cores)),
            dma((geo.bands, 2)),
        ],
        compiler_params=pltpu.CompilerParams(
            collective_id=0, has_side_effects=True, vmem_limit_bytes=60 * 2**20
        ),
    )(*args, *tables)


def assemble_kernel(isobars, run, got_ref, out_ref):
    bands = got_ref.shape[0]
    half_lat = WIN_LAT // 2
    groups = (isobars + 1) // 2
    rows = groups * 16
    whole_run = out_ref.shape[-1]
    tiles = whole_run // BLOCK
    extra = half_lat * run - BLOCK
    lane = lax.broadcasted_iota(jnp.int32, (rows, BLOCK), 1)

    @pl.loop(0, 2)
    def _(ih):
        for r in range(half_lat):
            out = [jnp.zeros((rows, BLOCK), F32) for _ in range(tiles)]
            for s in range(bands):
                base = s * run + run // 2
                piece = got_ref[s, ih].astype(F32)
                whole = min(run, BLOCK - r * run)
                parts = [(pltpu.roll(piece[:rows], (base - r * run) % BLOCK, 1), base, base + whole)]
                if whole < run:
                    rest = piece[rows:]
                    moved = [
                        pltpu.roll(rest, (base + whole - extra * k) % BLOCK, 1) for k in range(groups)
                    ]
                    parts.append((jnp.concatenate(moved, axis=0), base + whole, base + run))
                for value, low, high in parts:
                    spans = [(low, min(high, whole_run)), (max(low, whole_run) - whole_run, high - whole_run)]
                    for low, high in spans:
                        if high <= low:
                            continue
                        for t in range(low // BLOCK, (high - 1) // BLOCK + 1):
                            at = lane + t * BLOCK
                            out[t] = jnp.where(jnp.logical_and(at >= low, at < high), value, out[t])
            for t in range(tiles):
                value = out[t].reshape(2 * groups, 8, BLOCK)[:isobars]
                for flag in range(2):
                    top = ((half_lat if flag == 0 else 0) + r) * SQUARE_SPAN

                    @pl.when(ih == flag)
                    def _():
                        for v in range(2):
                            out_ref[v, :, top : top + SQUARE_SPAN, t * BLOCK : (t + 1) * BLOCK] = value[
                                :, v * SQUARE_SPAN : (v + 1) * SQUARE_SPAN
                            ]


def assemble(got, columns, isobars):
    bands = got.shape[0]
    run = columns * SQUARE_SPAN
    shape = (TARGET_QUANTITY // 2, isobars, WIN_LAT * SQUARE_SPAN, bands * run)
    return pl.pallas_call(
        functools.partial(assemble_kernel, isobars, run),
        out_shape=jax.ShapeDtypeStruct(shape, F32),
        compiler_params=pltpu.CompilerParams(vmem_limit_bytes=40 * 2**20),
    )(got)


def exchange(pieces, geo):
    half_lat = WIN_LAT // 2
    run = geo.cols * SQUARE_SPAN
    quantities = TARGET_QUANTITY // geo.cores
    rows = geo.slots * quantities * SQUARE_SPAN
    extra = half_lat * run - BLOCK
    lead = pieces.shape[:3]
    main = pieces[:, :, :, :rows].reshape(*lead, geo.slots, quantities, SQUARE_SPAN, BLOCK)
    rest = pieces[:, :, :, rows:, : extra * (geo.slots // 2)]
    rest = rest.reshape(*lead, 2, quantities, SQUARE_SPAN, geo.slots // 2, extra)
    rest = jnp.moveaxis(rest, 6, 3).reshape(*lead, geo.slots, quantities, SQUARE_SPAN, extra)
    maps = jnp.concatenate([main, rest], axis=-1)[:, :, :, : geo.isobars]
    maps = maps.reshape(*lead, geo.isobars, quantities, SQUARE_SPAN, half_lat, run)
    maps = jnp.transpose(maps, (2, 4, 3, 0, 1, 6, 5, 7))
    maps = maps.reshape(TARGET_QUANTITY, geo.isobars, geo.row_count * SQUARE_SPAN, run)
    maps = lax.all_to_all(maps, "var", split_axis=0, concat_axis=2, tiled=True)
    maps = jnp.roll(maps, half_lat * SQUARE_SPAN, 2)
    maps = lax.all_to_all(maps, "grid", split_axis=2, concat_axis=3, tiled=True)
    return jnp.roll(maps, run // 2, 3).astype(F32)


def local(
    tokens,
    key_mask,
    w_qkv,
    w_proj,
    w_up,
    w_down,
    level_query,
    w_dec_q,
    w_dec_kv,
    w_dec_o,
    decode_matrix,
):
    geo = Geometry(
        tokens, w_proj, level_query, decode_matrix, lax.axis_size("var"), lax.axis_size("grid")
    )
    pieces = forecast(
        geo,
        jnp.transpose(tokens, (1, 2, 0, 3)),
        key_mask.T,
        w_qkv,
        w_proj,
        w_up,
        w_down,
        level_query,
        w_dec_q,
        w_dec_kv,
        w_dec_o,
        decode_matrix.T,
    )
    if geo.scatter:
        return assemble(pieces, geo.cols, geo.isobars)
    return exchange(pieces, geo)


def solution(mesh):
    placed = (
        P("group", "grid", None, None),
        P("group", "grid"),
        P(None, None, "var"),
        P("var", None),
        P(None, "var"),
        P("var", None),
        P(),
        P(None, "var"),
        P(None, None, "var"),
        P("var", None),
        P(),
    )
    return jax.shard_map(
        local,
        mesh=mesh,
        in_specs=placed,
        out_specs=P("var", "group", "grid", None),
        check_vma=False,
    )
```

profile of v0, /device:TPU:0, one launch (start us, length us, event | category | flops | bytes accessed | tf_op | source)
XLA Modules:
  0.0 43.6 jit_solution(3208842640497547144)
XLA Ops:
  0.0 40.5 %shard_map.154.got_ref = bf16[8,2,128,128]{3,2,1,0:T(8,128)(2,1)} custom-call(bf16[12,3,48,512]{3,2,1,0:T(8,128)(2,1)} %bitcast.3, s32[12,48]{1,0:T(8,128)} %bitcast.5, bf16[3,512,256]{2,1,0:T(8,128)(2,1)} %wqkv_ref.1, bf16[256,512]{1,0:T(8,128)(2,1)} %wproj_ref.1, bf16[512,1024]{1,0:T(8,128)(2,1)} %wup_ref.1, bf16[1024,512]{1,0:T(8,128)(2,1)} %wdown_ref.1, ...), custom_call_target="tpu_custom_call" | custom-call | tf_op jit(solution)/shard_map/pallas_call | solution.py:523
  40.6 0.0 copy-start
  40.6 1.0 %copy-done = bf16[8,2,128,128]{3,2,1,0:T(8,128)(2,1)S(1)} copy-done((bf16[8,2,128,128]{3,2,1,0:T(8,128)(2,1)S(1)}, bf16[8,2,128,128]{3,2,1,0:T(8,128)(2,1)}, u32[]{:S(2)}) %copy-start) | copy-done | bytes 524312
  41.6 2.0 %shard_map.155 = f32[2,13,24,384]{3,2,1,0:T(8,128)} custom-call(bf16[8,2,128,128]{3,2,1,0:T(8,128)(2,1)S(1)} %copy-done), custom_call_target="tpu_custom_call" | custom-call | tf_op jit(solution)/shard_map/pallas_call | solution.py:613
Async XLA Ops:
  40.6 1.0 %copy-start = (bf16[8,2,128,128]{3,2,1,0:T(8,128)(2,1)S(1)}, bf16[8,2,128,128]{3,2,1,0:T(8,128)(2,1)}, u32[]{:S(2)}) copy-start(bf16[8,2,128,128]{3,2,1,0:T(8,128)(2,1)} %shard_map.154.got_ref) | copy-start | bytes 1572868
where the time goes:
time: 44.2 us; the launch traced here: 43.6 us
  Pallas kernels  42.5 us (96%)
  local copies, waits for them, and re-layouts  1.03 us (2%)
    pallas_call x1, Pallas kernels, forecast(): pl.pallas_call(functools.partial(main_kernel, geo), out_shape=jax.ShapeDt...  40.5 us
    pallas_call x1, Pallas kernels, assemble(): pl.pallas_call(functools.partial(assemble_kernel, isobars, run), out_shap...  1.97 us
    unnamed x2, local copies, waits for them, and re-layouts  1.03 us

commit v1 on v0

--- a/solution.py
+++ b/solution.py
@@ -68,10 +68,12 @@
         return table.reshape(self.windows * self.half, -1)
 
     def order_table(self):
-        table = np.zeros((KEYS, self.tokens), np.float32)
+        table = np.zeros((self.levels * BLOCK, self.tokens), np.float32)
         for half, level, r, c in self.each():
             patch = r * self.cols + half * self.half_cols + c
-            table[level * self.patches + patch, self.place(half, level, r, c)] = 1.0
+            table[level * BLOCK + patch, self.place(half, level, r, c)] = 1.0
+            if level > 0:
+                table[level * BLOCK + patch, self.place(half, 0, r, c)] = -1.0
         return table
 
     def position_table(self):
@@ -96,14 +98,18 @@
     def pick_table(self):
         half_lat = WIN_LAT // 2
         run = self.cols * SQUARE_SPAN
-        picks = np.zeros((SQUARE_SPAN, BLOCK, 3 * BLOCK), np.float32)
+        extra = half_lat * run - BLOCK
+        picks = np.zeros((SQUARE_SPAN, BLOCK, 4 * BLOCK), np.float32)
         for ih in range(2):
             for q in range(half_lat * run):
                 r, rest = divmod(q, run)
                 column, b = divmod(rest, SQUARE_SPAN)
                 source = (half_lat * ih + r) * self.cols + column
-                target = ih * BLOCK + q if q < BLOCK else 2 * BLOCK + ih * (BLOCK // 2) + q - BLOCK
-                picks[b, source, target] = 1.0
+                if q < BLOCK:
+                    picks[b, source, ih * BLOCK + q] = 1.0
+                else:
+                    for k in range(self.slots // 2):
+                        picks[b, source, (2 + ih) * BLOCK + extra * k + q - BLOCK] = 1.0
         return picks
 
 
@@ -191,7 +197,8 @@
     hid,
     dw,
     du,
-    base_pix,
+    fold_base,
+    x_one,
     pix,
     pieces,
     checked,
@@ -301,9 +308,7 @@
         pos = jnp.where(pos >= half, pos - half, pos)
         for level in range(levels - 1, 0, -1):
             start = geo.half_patches * level
-            pos = jnp.where(pos >= start, pos - geo.half_patches, pos) if level == 1 else jnp.where(
-                pos >= start, pos - start, pos
-            )
+            pos = jnp.where(pos >= start, pos - start, pos)
         return pos >= geo.half_patches // 2
 
     differs[...] = jnp.where(region_of(q_pos) != region_of(k_pos), -1e30, 0.0)
@@ -313,17 +318,15 @@
     for copy in late_loads:
         copy.wait()
     copies.append(remote(fold.at[0], fold.at[1], weight_send.at[5], weight_recv.at[5], sibling))
-    for copy in copies:
-        copy.wait()
 
     count = heads * LEVEL_SLOTS
     pixels = geo.pixels
-    patches = geo.patches
     row_size = pixels // cores // SQUARE_SPAN
     rows = geo.slots * row_size
     half_lat = WIN_LAT // 2
     extra = half_lat * geo.cols * SQUARE_SPAN - BLOCK
     pair = 8 // heads
+    units = up.shape[2]
 
     def piece_copy(w, ih, core, action):
         band = lax.rem(var * windows + w + ih, bands)
@@ -349,9 +352,16 @@
             else:
                 pltpu.make_async_copy(source, source, piece_send.at[w, ih, core]).wait()
 
-    @pl.loop(0, windows)
-    def _(w):
+    def arrive(w):
         pltpu.make_async_copy(halo.at[w], halo.at[w], halo_recv.at[w]).wait()
+
+    def send(w):
+        if geo.scatter:
+            for ih in range(2):
+                for core in range(cores):
+                    piece_copy(w, ih, core, "start")
+
+    def attend(w):
         x = jnp.concatenate([own[w], halo[w]], axis=0).astype(F32)
         n1 = layer_norm(x).astype(BF16)
         target = position[0:1, :] + (var * geo.row_count + WIN_LAT * w + half_lat)
@@ -368,7 +378,7 @@
         allowed = jnp.logical_or(jnp.broadcast_to(opened, diagonal.shape) > 0.5, diagonal)
         cut = jnp.logical_and(var == cores - 1, w == windows - 1)
         bias = jnp.where(allowed, 0.0, -1e30) + differs[...] * jnp.where(cut, 1.0, 0.0)
-        attended = jnp.zeros((tokens, features), F32)
+        attended = x
         for s in range(cores):
             q = jnp.dot(n1, qkv[s, 0], preferred_element_type=F32).astype(BF16)
             q = q * jnp.asarray(HD ** (-0.5), BF16)
@@ -394,61 +404,40 @@
             )
             context = jnp.dot(weights, v_all, preferred_element_type=F32).astype(BF16)
             attended = attended + jnp.dot(context, proj[s], preferred_element_type=F32)
-        x_one = x + attended
-        n2 = layer_norm(x_one).astype(BF16)
-        units = up.shape[2]
+        x_one[w] = attended
+
+    def finish(w):
+        n2 = layer_norm(x_one[w]).astype(BF16)
         for s in range(cores):
             for c in range(0, units, CHUNK):
                 one = jnp.dot(n2, up[s, :, c : c + CHUNK], preferred_element_type=F32)
                 one = 0.5 * one * (1.0 + lax.erf(one * 2.0 ** (-0.5)))
                 hid[:, s * units + c : s * units + c + CHUNK] = one.astype(BF16)
-        latent = x_one + jnp.dot(
+        latent = x_one[w] + jnp.dot(
             hid[...], down[...].reshape(cores * units, features), preferred_element_type=F32
         )
         n3 = layer_norm(latent.astype(BF16).astype(F32)).astype(BF16)
         n3 = jnp.dot(order[...], n3, preferred_element_type=F32).astype(BF16)
-
-        lane = lax.broadcasted_iota(jnp.int32, (1, BLOCK), 1)
-
-        def by_level(value):
-            low, high = value[:, :BLOCK], value[:, BLOCK:]
-            found = []
-            for level in range(levels):
-                start = level * patches
-                if start < BLOCK:
-                    part = low if start == 0 else pltpu.roll(low, BLOCK - start, 1)
-                    if start + patches > BLOCK:
-                        part = jnp.where(lane < BLOCK - start, part, pltpu.roll(high, BLOCK - start, 1))
-                else:
-                    part = pltpu.roll(high, 2 * BLOCK - start, 1) if start > BLOCK else high
-                found.append(part)
-            return found
-
-        base = jnp.zeros((pixels, BLOCK), F32)
+        n3, others = n3[:BLOCK], n3[BLOCK:]
+        base = lax.dot_general(fold_base[...], n3, NT, preferred_element_type=F32)
+        base = base[:pixels] + base[pixels:]
         for s in range(cores):
-            g = lax.dot_general(fold[s, 0 : 2 * count, :], n3, NT, preferred_element_type=F32)
-            scores = by_level(g[:count] + g[count:])
+            g = lax.dot_general(fold[s, 0 : 2 * count, :], others, NT, preferred_element_type=F32)
+            g = g[:count] + g[count:]
+            scores = [jnp.zeros((count, BLOCK), F32)]
+            scores += [g[:, j * BLOCK : (j + 1) * BLOCK] for j in range(levels - 1)]
             peak = functools.reduce(jnp.maximum, scores)
             e = [jnp.exp(one - peak) for one in scores]
             inverse = 1.0 / sum(e)
-            for j in range(1, levels):
-                dw[j - 1, s * count : (s + 1) * count, :] = e[j] * inverse
-            u = by_level(
-                lax.dot_general(fold[s, 2 * count :, :], n3, NT, preferred_element_type=F32)
-            )
-            for h in range(heads):
-                base = base + u[0][h * pixels : (h + 1) * pixels]
-            for j in range(1, levels):
-                du[j - 1, s * heads * pixels : (s + 1) * heads * pixels, :] = u[j] - u[0]
-        base_pix[...] = base
-
-        @pl.loop(0, geo.slots // pair)
-        def _(at):
-            totals = [base_pix[...] for _ in range(pair)]
+            u = lax.dot_general(fold[s, 2 * count :, :], others, NT, preferred_element_type=F32)
+            for j in range(levels - 1):
+                dw[j, s * count : (s + 1) * count, :] = e[j + 1] * inverse
+                du[j, s * heads * pixels : (s + 1) * heads * pixels, :] = u[:, j * BLOCK : (j + 1) * BLOCK]
+        for at in range(geo.slots // pair):
+            totals = [base for _ in range(pair)]
             for s in range(cores):
                 for j in range(levels - 1):
-                    start = pl.multiple_of(s * count + at * 8, 8)
-                    some = dw[j, pl.ds(start, 8), :]
+                    some = dw[j, s * count + at * 8 : s * count + at * 8 + 8, :]
                     for h in range(heads):
                         top = (s * heads + h) * pixels
                         value = du[j, top : top + pixels, :]
@@ -456,10 +445,9 @@
                             totals[n] = totals[n] + some[n * heads + h : n * heads + h + 1] * value
             for n in range(pair):
                 pix[at * pair + n] = totals[n]
-
         lane = lax.broadcasted_iota(jnp.int32, (2 * row_size, BLOCK), 1)
         for core in range(cores):
-            total = jnp.zeros((rows, 3 * BLOCK), F32)
+            total = jnp.zeros((rows, 4 * BLOCK), F32)
             for b in range(SQUARE_SPAN):
                 top = (core * SQUARE_SPAN + b) * row_size
                 part = pix[:, top : top + row_size, :].reshape(rows, BLOCK)
@@ -468,18 +456,37 @@
                 left = jnp.zeros((2 * row_size, BLOCK), F32)
                 for k in range(geo.slots // 2):
                     at = slice(2 * row_size * k, 2 * row_size * (k + 1))
-                    moved = pltpu.roll(
-                        total[at, 2 * BLOCK :], (extra * k - (BLOCK // 2) * ih) % BLOCK, 1
-                    )
                     inside = jnp.logical_and(lane >= extra * k, lane < extra * (k + 1))
-                    left = jnp.where(inside, moved, left)
+                    left = jnp.where(inside, total[at, (2 + ih) * BLOCK : (3 + ih) * BLOCK], left)
                 main = total[:, ih * BLOCK : (ih + 1) * BLOCK]
                 pieces[w, ih, core] = jnp.concatenate([main, left], axis=0).astype(BF16)
-        if geo.scatter:
-            checked[...] = pieces[w].astype(F32).max(axis=(0, 1))
-            for ih in range(2):
-                for core in range(cores):
-                    piece_copy(w, ih, core, "start")
+        checked[...] = pieces[w].astype(F32).max(axis=(0, 1))
+
+    mask_copy, qkv_copy, proj_copy, up_copy, down_copy, fold_copy = copies
+    for copy in (mask_copy, qkv_copy, proj_copy):
+        copy.wait()
+    arrive(0)
+    attend(0)
+    for copy in (up_copy, down_copy, fold_copy):
+        copy.wait()
+    whole = jnp.zeros((pixels, features), F32)
+    for s in range(cores):
+        for h in range(heads):
+            top = 2 * count + h * pixels
+            whole = whole + fold[s, top : top + pixels, :].astype(F32)
+    whole_hi = whole.astype(BF16)
+    fold_base[0:pixels, :] = whole_hi
+    fold_base[pixels:, :] = (whole - whole_hi.astype(F32)).astype(BF16)
+
+    @pl.loop(0, windows - 1)
+    def _(w):
+        arrive(w + 1)
+        finish(w)
+        attend(w + 1)
+        send(w)
+
+    finish(windows - 1)
+    send(windows - 1)
 
     for copy in halos:
         copy.wait_send()
@@ -542,7 +549,8 @@
             vmem((geo.tokens, cores * units), BF16),
             vmem((geo.levels - 1, cores * geo.heads * LEVEL_SLOTS, BLOCK), F32),
             vmem((geo.levels - 1, cores * geo.heads * geo.pixels, BLOCK), F32),
-            vmem((geo.pixels, BLOCK), F32),
+            vmem((2 * geo.pixels, features), BF16),
+            vmem((windows, geo.tokens, features), F32),
             vmem((geo.slots, geo.pixels, BLOCK), F32),
             vmem((windows, 2, cores, BLOCK, BLOCK), BF16),
             vmem((BLOCK, BLOCK), F32),

time: 44.2 us -> 41.5 us (0.939)
  Pallas kernels: 42.5 us -> 40.1 us
    pallas_call x1, Pallas kernels: 40.5 us -> 38.1 us  [forecast(): pl.pallas_call(functools.partial(main_kernel, geo), out_shape=jax.ShapeDt...]
where the time goes in v1:
time: 41.5 us; the launch traced here: 41.1 us
  Pallas kernels  40.1 us (97%)
  local copies, waits for them, and re-layouts  1.03 us (2%)
    pallas_call x1, Pallas kernels, forecast(): pl.pallas_call(functools.partial(main_kernel, geo), out_shape=jax.ShapeDt...  38.1 us
    pallas_call x1, Pallas kernels, assemble(): pl.pallas_call(functools.partial(assemble_kernel, isobars, run), out_shap...  1.97 us
    unnamed x2, local copies, waits for them, and re-layouts  1.03 us

profile of v1, /device:TPU:0, one launch (start us, length us, event | category | flops | bytes accessed | tf_op | source)
XLA Modules:
  0.0 41.1 jit_solution(16354802425190164479)
XLA Ops:
  0.0 38.1 %shard_map.154.got_ref = bf16[8,2,128,128]{3,2,1,0:T(8,128)(2,1)} custom-call(bf16[12,3,48,512]{3,2,1,0:T(8,128)(2,1)} %bitcast.3, s32[12,48]{1,0:T(8,128)} %bitcast.5, bf16[3,512,256]{2,1,0:T(8,128)(2,1)} %wqkv_ref.1, bf16[256,512]{1,0:T(8,128)(2,1)} %wproj_ref.1, bf16[512,1024]{1,0:T(8,128)(2,1)} %wup_ref.1, bf16[1024,512]{1,0:T(8,128)(2,1)} %wdown_ref.1, ...), custom_call_target="tpu_custom_call" | custom-call | tf_op jit(solution)/shard_map/pallas_call | solution.py:530
  38.1 0.0 copy-start
  38.1 1.0 %copy-done = bf16[8,2,128,128]{3,2,1,0:T(8,128)(2,1)S(1)} copy-done((bf16[8,2,128,128]{3,2,1,0:T(8,128)(2,1)S(1)}, bf16[8,2,128,128]{3,2,1,0:T(8,128)(2,1)}, u32[]{:S(2)}) %copy-start) | copy-done | bytes 524312
  39.2 2.0 %shard_map.155 = f32[2,13,24,384]{3,2,1,0:T(8,128)} custom-call(bf16[8,2,128,128]{3,2,1,0:T(8,128)(2,1)S(1)} %copy-done), custom_call_target="tpu_custom_call" | custom-call | tf_op jit(solution)/shard_map/pallas_call | solution.py:621
Async XLA Ops:
  38.1 1.0 %copy-start = (bf16[8,2,128,128]{3,2,1,0:T(8,128)(2,1)S(1)}, bf16[8,2,128,128]{3,2,1,0:T(8,128)(2,1)}, u32[]{:S(2)}) copy-start(bf16[8,2,128,128]{3,2,1,0:T(8,128)(2,1)} %shard_map.154.got_ref) | copy-start | bytes 1572868

commit v2 on v1

--- a/solution.py
+++ b/solution.py
@@ -17,6 +17,7 @@
 KEYS = 256
 CHUNK = 256
 LEVEL_SLOTS = 16
+ORDER = "abaabbbbaaabbbbabaabbbb"
 MESH = pl.DeviceIdType.MESH
 NT = (((1,), (1,)), ((), ()))
 F32 = jnp.float32
@@ -70,7 +71,7 @@
     def order_table(self):
         table = np.zeros((self.levels * BLOCK, self.tokens), np.float32)
         for half, level, r, c in self.each():
-            patch = r * self.cols + half * self.half_cols + c
+            patch = r * self.cols + (1 - half) * self.half_cols + c
             table[level * BLOCK + patch, self.place(half, level, r, c)] = 1.0
             if level > 0:
                 table[level * BLOCK + patch, self.place(half, 0, r, c)] = -1.0
@@ -82,7 +83,7 @@
         for half, level, r, c in self.each():
             at = self.place(half, level, r, c)
             table[0, at] = r
-            table[1 + half, at] = c + (self.half_cols if half == 0 else 0)
+            table[1 + half, at] = c + half * self.half_cols
         return table
 
     def pixel_table(self):
@@ -199,6 +200,7 @@
     du,
     fold_base,
     x_one,
+    base_pix,
     pix,
     pieces,
     checked,
@@ -214,8 +216,13 @@
     bands, cores, windows, half = geo.bands, geo.cores, geo.windows, geo.half
     features, levels, width, heads = geo.features, geo.levels, geo.width, geo.heads
     sibling = (group, grid, lax.rem(var + 1, cores))
+
+    def turn(step, column=grid):
+        return lax.rem(column + step + 1, windows)
+
+    east_grid = lax.rem(grid + 1, bands)
     west = (group, lax.rem(grid + bands - 1, bands), var)
-    east = (group, lax.rem(grid + 1, bands), var)
+    east = (group, east_grid, var)
     barrier = pltpu.get_barrier_semaphore()
     if geo.scatter:
         peers = bands * cores
@@ -242,15 +249,20 @@
         loads.append(copy)
         return copy
 
+    gather_load = load(gather_ref, gather)
     tiles = geo.rows // 8
     first_tile = var * (geo.row_count // 8)
     slabs = []
     for s in range(geo.taken // 8):
         tile = lax.rem(first_tile + s, tiles)
-        slabs.append(
-            load(tok_ref.at[:, :, pl.ds(pl.multiple_of(tile * 8, 8), 8), :], raw.at[:, :, 8 * s : 8 * s + 8, :])
-        )
-    gather_load = load(gather_ref, gather)
+        for h in (0, 1):
+            some = slice(h * geo.half_cols, (h + 1) * geo.half_cols)
+            slabs.append(
+                load(
+                    tok_ref.at[some, :, pl.ds(pl.multiple_of(tile * 8, 8), 8), :],
+                    raw.at[some, :, 8 * s : 8 * s + 8, :],
+                )
+            )
     fold_loads = [
         load(a, b)
         for a, b in ((lq_ref, lq), (wq_ref, wq), (wkv_ref, wkv), (wo_ref, wo), (dm_ref, dm), (perm_ref, perm))
@@ -269,16 +281,17 @@
         )
     ]
 
-    for copy in slabs:
+    depth = geo.half_cols * levels * geo.taken
+
+    def collect(h, w, target):
+        slab = raw[h * geo.half_cols : (h + 1) * geo.half_cols].reshape(depth, features)
+        picked = gather[pl.ds(pl.multiple_of(w * half, 16), half), :]
+        target[w] = jnp.dot(picked, slab, preferred_element_type=F32).astype(BF16)
+
+    gather_load.wait()
+    for copy in slabs[1::2]:
         copy.wait()
-    gather_load.wait()
-    depth = geo.half_cols * levels * geo.taken
-    for h, target in ((0, first), (1, own)):
-        slab = raw[h * geo.half_cols : (h + 1) * geo.half_cols].reshape(depth, features)
-        for c in range(0, features, CHUNK):
-            rows = jnp.dot(gather[...], slab[:, c : c + CHUNK], preferred_element_type=F32).astype(BF16)
-            target[:, :, c : c + CHUNK] = rows.reshape(windows, half, CHUNK)
-
+    collect(1, turn(0, east_grid), first)
     pl.semaphore_wait(barrier, greeted)
 
     def remote(source, target, send, recv, peer):
@@ -288,13 +301,25 @@
         copy.start()
         return copy
 
-    copies = [remote(mask_ref, marks.at[1], weight_send.at[0], weight_recv.at[0], west)]
+    copies = [remote(mask_ref, marks.at[1], weight_send.at[0], weight_recv.at[0], east)]
     halos = []
-    for w in range(windows):
-        halos.append(remote(first.at[w], halo.at[w], halo_send.at[w], halo_recv.at[w], west))
+
+    def pass_on(step):
+        w = turn(step, east_grid)
+        halos.append(remote(first.at[w], halo.at[w], halo_send.at[w], halo_recv.at[w], east))
+
+    pass_on(0)
     for n, (source, target) in enumerate(((wqkv_ref, qkv), (wproj_ref, proj), (wup_ref, up), (wdown_ref, down))):
         copies.append(remote(source, target.at[1], weight_send.at[n + 1], weight_recv.at[n + 1], sibling))
 
+    for step in range(1, windows):
+        collect(1, turn(step, east_grid), first)
+    for copy in slabs[0::2]:
+        copy.wait()
+    for step in range(windows):
+        collect(0, turn(step), own)
+    for step in range(1, windows):
+        pass_on(step)
     for copy in fold_loads:
         copy.wait()
     fold_decoder(lq[...], wq[...], wkv, wo[...], dm[...], perm[...], fold)
@@ -325,7 +350,7 @@
     rows = geo.slots * row_size
     half_lat = WIN_LAT // 2
     extra = half_lat * geo.cols * SQUARE_SPAN - BLOCK
-    pair = 8 // heads
+    pix[geo.isobars :] = jnp.zeros((geo.slots - geo.isobars, pixels, BLOCK), F32)
     units = up.shape[2]
 
     def piece_copy(w, ih, core, action):
@@ -355,10 +380,12 @@
     def arrive(w):
         pltpu.make_async_copy(halo.at[w], halo.at[w], halo_recv.at[w]).wait()
 
-    def send(w):
+    def send(w, some=range(cores)):
+        for core in some:
+            checked[...] = pieces[w, :, core].astype(F32).max(axis=0)
         if geo.scatter:
-            for ih in range(2):
-                for core in range(cores):
+            for core in some:
+                for ih in range(2):
                     piece_copy(w, ih, core, "start")
 
     def attend(w):
@@ -378,7 +405,8 @@
         allowed = jnp.logical_or(jnp.broadcast_to(opened, diagonal.shape) > 0.5, diagonal)
         cut = jnp.logical_and(var == cores - 1, w == windows - 1)
         bias = jnp.where(allowed, 0.0, -1e30) + differs[...] * jnp.where(cut, 1.0, 0.0)
-        attended = x
+        yield
+        scores, values = [], []
         for s in range(cores):
             q = jnp.dot(n1, qkv[s, 0], preferred_element_type=F32).astype(BF16)
             q = q * jnp.asarray(HD ** (-0.5), BF16)
@@ -386,41 +414,53 @@
             v = jnp.dot(n1, qkv[s, 2], preferred_element_type=F32).astype(BF16)
             tail = jnp.zeros((KEYS - tokens, width), BF16)
             k = jnp.concatenate([k, tail], axis=0)
-            v = jnp.concatenate([v, tail], axis=0)
+            values.append(jnp.concatenate([v, tail], axis=0))
             q_all = jnp.concatenate(
                 [jnp.where(lane_head == h, q, jnp.zeros_like(q)) for h in range(heads)], axis=0
             )
-            scores = lax.dot_general(q_all, k, NT, preferred_element_type=F32)
+            yield
+            scores.append(lax.dot_general(q_all, k, NT, preferred_element_type=F32))
+            yield
+        attended = x
+        for s in range(cores):
             weights = []
             for h in range(heads):
-                one = scores[h * tokens : (h + 1) * tokens] + bias
+                one = scores[s][h * tokens : (h + 1) * tokens] + bias
                 peak = jnp.max(one, axis=-1, keepdims=True)
                 e = jnp.exp(one - peak)
                 total = jnp.sum(e, axis=-1, keepdims=True)
                 weights.append((e * (1.0 / total)).astype(BF16))
             weights = jnp.concatenate(weights, axis=1)
+            v = values[s]
             v_all = jnp.concatenate(
                 [jnp.where(lane_head_keys == h, v, jnp.zeros_like(v)) for h in range(heads)], axis=0
             )
             context = jnp.dot(weights, v_all, preferred_element_type=F32).astype(BF16)
+            yield
             attended = attended + jnp.dot(context, proj[s], preferred_element_type=F32)
-        x_one[w] = attended
+            if s == cores - 1:
+                x_one[w] = attended
+            yield
 
     def finish(w):
         n2 = layer_norm(x_one[w]).astype(BF16)
+        yield
         for s in range(cores):
             for c in range(0, units, CHUNK):
                 one = jnp.dot(n2, up[s, :, c : c + CHUNK], preferred_element_type=F32)
                 one = 0.5 * one * (1.0 + lax.erf(one * 2.0 ** (-0.5)))
                 hid[:, s * units + c : s * units + c + CHUNK] = one.astype(BF16)
+                yield
         latent = x_one[w] + jnp.dot(
             hid[...], down[...].reshape(cores * units, features), preferred_element_type=F32
         )
+        yield
         n3 = layer_norm(latent.astype(BF16).astype(F32)).astype(BF16)
         n3 = jnp.dot(order[...], n3, preferred_element_type=F32).astype(BF16)
         n3, others = n3[:BLOCK], n3[BLOCK:]
+        yield
         base = lax.dot_general(fold_base[...], n3, NT, preferred_element_type=F32)
-        base = base[:pixels] + base[pixels:]
+        base_pix[...] = base[:pixels] + base[pixels:]
         for s in range(cores):
             g = lax.dot_general(fold[s, 0 : 2 * count, :], others, NT, preferred_element_type=F32)
             g = g[:count] + g[count:]
@@ -433,24 +473,30 @@
             for j in range(levels - 1):
                 dw[j, s * count : (s + 1) * count, :] = e[j + 1] * inverse
                 du[j, s * heads * pixels : (s + 1) * heads * pixels, :] = u[:, j * BLOCK : (j + 1) * BLOCK]
-        for at in range(geo.slots // pair):
-            totals = [base for _ in range(pair)]
-            for s in range(cores):
-                for j in range(levels - 1):
-                    some = dw[j, s * count + at * 8 : s * count + at * 8 + 8, :]
-                    for h in range(heads):
-                        top = (s * heads + h) * pixels
-                        value = du[j, top : top + pixels, :]
-                        for n in range(pair):
-                            totals[n] = totals[n] + some[n * heads + h : n * heads + h + 1] * value
-            for n in range(pair):
-                pix[at * pair + n] = totals[n]
+        yield
+
+    def paint(w):
+        low = pixels // cores
         lane = lax.broadcasted_iota(jnp.int32, (2 * row_size, BLOCK), 1)
         for core in range(cores):
+            top = core * low
+            for first_level in range(0, geo.isobars, 5):
+                some = range(first_level, min(first_level + 5, geo.isobars))
+                totals = [base_pix[top : top + low, :] for _ in some]
+                for s in range(cores):
+                    for h in range(heads):
+                        for j in range(levels - 1):
+                            at = (s * heads + h) * pixels + top
+                            value = du[j, at : at + low, :]
+                            for n, level in enumerate(some):
+                                row = s * count + level * heads + h
+                                totals[n] = totals[n] + dw[j, row : row + 1, :] * value
+                for n, level in enumerate(some):
+                    pix[level, top : top + low, :] = totals[n]
             total = jnp.zeros((rows, 4 * BLOCK), F32)
             for b in range(SQUARE_SPAN):
-                top = (core * SQUARE_SPAN + b) * row_size
-                part = pix[:, top : top + row_size, :].reshape(rows, BLOCK)
+                at = top + b * row_size
+                part = pix[:, at : at + row_size, :].reshape(rows, BLOCK)
                 total = total + jnp.dot(part.astype(BF16), pick[b], preferred_element_type=F32)
             for ih in range(2):
                 left = jnp.zeros((2 * row_size, BLOCK), F32)
@@ -460,13 +506,17 @@
                     left = jnp.where(inside, total[at, (2 + ih) * BLOCK : (3 + ih) * BLOCK], left)
                 main = total[:, ih * BLOCK : (ih + 1) * BLOCK]
                 pieces[w, ih, core] = jnp.concatenate([main, left], axis=0).astype(BF16)
-        checked[...] = pieces[w].astype(F32).max(axis=(0, 1))
+            yield
+
+    def run(order="", **steps):
+        for name in order:
+            next(steps[name])
 
     mask_copy, qkv_copy, proj_copy, up_copy, down_copy, fold_copy = copies
     for copy in (mask_copy, qkv_copy, proj_copy):
         copy.wait()
-    arrive(0)
-    attend(0)
+    arrive(turn(0))
+    run("a" * ORDER.count("a"), a=attend(turn(0)))
     for copy in (up_copy, down_copy, fold_copy):
         copy.wait()
     whole = jnp.zeros((pixels, features), F32)
@@ -478,15 +528,23 @@
     fold_base[0:pixels, :] = whole_hi
     fold_base[pixels:, :] = (whole - whole_hi.astype(F32)).astype(BF16)
 
-    @pl.loop(0, windows - 1)
-    def _(w):
-        arrive(w + 1)
-        finish(w)
-        attend(w + 1)
-        send(w)
-
-    finish(windows - 1)
-    send(windows - 1)
+    last = windows - 1
+
+    def complete(w):
+        yield from finish(w)
+        yield from paint(w)
+
+    @pl.loop(0, last)
+    def _(step):
+        arrive(turn(step + 1))
+        run(ORDER, a=attend(turn(step + 1)), b=complete(turn(step)))
+        send(turn(step))
+
+    finishing = complete(turn(last))
+    run("b" * (ORDER.count("b") - cores), b=finishing)
+    for core in range(cores):
+        next(finishing)
+        send(turn(last), (core,))
 
     for copy in halos:
         copy.wait_send()
@@ -551,10 +609,11 @@
             vmem((geo.levels - 1, cores * geo.heads * geo.pixels, BLOCK), F32),
             vmem((2 * geo.pixels, features), BF16),
             vmem((windows, geo.tokens, features), F32),
+            vmem((geo.pixels, BLOCK), F32),
             vmem((geo.slots, geo.pixels, BLOCK), F32),
             vmem((windows, 2, cores, BLOCK, BLOCK), BF16),
             vmem((BLOCK, BLOCK), F32),
-            dma((geo.taken // 8 + 15,)),
+            dma((geo.taken // 4 + 15,)),
             dma((6,)),
             dma((6,)),
             dma((windows,)),
@@ -583,7 +642,7 @@
         for r in range(half_lat):
             out = [jnp.zeros((rows, BLOCK), F32) for _ in range(tiles)]
             for s in range(bands):
-                base = s * run + run // 2
+                base = (s * run + whole_run - run // 2) % whole_run
                 piece = got_ref[s, ih].astype(F32)
                 whole = min(run, BLOCK - r * run)
                 parts = [(pltpu.roll(piece[:rows], (base - r * run) % BLOCK, 1), base, base + whole)]
@@ -643,7 +702,7 @@
     maps = lax.all_to_all(maps, "var", split_axis=0, concat_axis=2, tiled=True)
     maps = jnp.roll(maps, half_lat * SQUARE_SPAN, 2)
     maps = lax.all_to_all(maps, "grid", split_axis=2, concat_axis=3, tiled=True)
-    return jnp.roll(maps, run // 2, 3).astype(F32)
+    return jnp.roll(maps, -(run // 2), 3).astype(F32)
 
 
 def local(

time: 41.5 us -> 37.9 us (0.913)
  Pallas kernels: 40.1 us -> 36.7 us
    pallas_call x1, Pallas kernels: 38.1 us -> 34.7 us  [forecast(): pl.pallas_call(functools.partial(main_kernel, geo), out_shape=jax.ShapeDt...]
where the time goes in v2:
time: 37.9 us; the launch traced here: 37.7 us
  Pallas kernels  36.7 us (97%)
  local copies, waits for them, and re-layouts  1.03 us (3%)
    pallas_call x1, Pallas kernels, forecast(): pl.pallas_call(functools.partial(main_kernel, geo), out_shape=jax.ShapeDt...  34.7 us
    pallas_call x1, Pallas kernels, assemble(): pl.pallas_call(functools.partial(assemble_kernel, isobars, run), out_shap...  1.97 us
    unnamed x2, local copies, waits for them, and re-layouts  1.03 us

profile of v2, /device:TPU:0, one launch (start us, length us, event | category | flops | bytes accessed | tf_op | source)
XLA Modules:
  0.0 37.7 jit_solution(2426078670842095788)
XLA Ops:
  0.0 34.7 %shard_map.154.got_ref = bf16[8,2,128,128]{3,2,1,0:T(8,128)(2,1)} custom-call(bf16[12,3,48,512]{3,2,1,0:T(8,128)(2,1)} %bitcast.3, s32[12,48]{1,0:T(8,128)} %bitcast.5, bf16[3,512,256]{2,1,0:T(8,128)(2,1)} %wqkv_ref.1, bf16[256,512]{1,0:T(8,128)(2,1)} %wproj_ref.1, bf16[512,1024]{1,0:T(8,128)(2,1)} %wup_ref.1, bf16[1024,512]{1,0:T(8,128)(2,1)} %wdown_ref.1, ...), custom_call_target="tpu_custom_call" | custom-call | tf_op jit(solution)/shard_map/pallas_call | solution.py:588
  34.7 0.0 copy-start
  34.7 1.0 %copy-done = bf16[8,2,128,128]{3,2,1,0:T(8,128)(2,1)S(1)} copy-done((bf16[8,2,128,128]{3,2,1,0:T(8,128)(2,1)S(1)}, bf16[8,2,128,128]{3,2,1,0:T(8,128)(2,1)}, u32[]{:S(2)}) %copy-start) | copy-done | bytes 524312
  35.8 2.0 %shard_map.155 = f32[2,13,24,384]{3,2,1,0:T(8,128)} custom-call(bf16[8,2,128,128]{3,2,1,0:T(8,128)(2,1)S(1)} %copy-done), custom_call_target="tpu_custom_call" | custom-call | tf_op jit(solution)/shard_map/pallas_call | solution.py:680
Async XLA Ops:
  34.7 1.0 %copy-start = (bf16[8,2,128,128]{3,2,1,0:T(8,128)(2,1)S(1)}, bf16[8,2,128,128]{3,2,1,0:T(8,128)(2,1)}, u32[]{:S(2)}) copy-start(bf16[8,2,128,128]{3,2,1,0:T(8,128)(2,1)} %shard_map.154.got_ref) | copy-start | bytes 1572868

commit v3 on v2

--- a/solution.py
+++ b/solution.py
@@ -198,6 +198,7 @@
     hid,
     dw,
     du,
+    ready,
     fold_base,
     x_one,
     base_pix,
@@ -218,7 +219,9 @@
     sibling = (group, grid, lax.rem(var + 1, cores))
 
     def turn(step, column=grid):
-        return lax.rem(column + step + 1, windows)
+        near = column * cores // bands == var
+        rest = lax.rem(step + column + windows - 2, windows - 1)
+        return jnp.where(near, jnp.where(step == 0, windows - 1, rest), step)
 
     east_grid = lax.rem(grid + 1, bands)
     west = (group, lax.rem(grid + bands - 1, bands), var)
@@ -390,7 +393,7 @@
 
     def attend(w):
         x = jnp.concatenate([own[w], halo[w]], axis=0).astype(F32)
-        n1 = layer_norm(x).astype(BF16)
+        n1 = layer_norm(x[half:]).astype(BF16)
         target = position[0:1, :] + (var * geo.row_count + WIN_LAT * w + half_lat)
         target = jnp.where(target >= geo.rows, target - geo.rows, target)
         there = lax.broadcasted_iota(jnp.int32, (geo.rows, KEYS), 0) == target
@@ -408,10 +411,13 @@
         yield
         scores, values = [], []
         for s in range(cores):
-            q = jnp.dot(n1, qkv[s, 0], preferred_element_type=F32).astype(BF16)
+            q, k, v = (
+                jnp.concatenate(
+                    [ready[s, i, w], jnp.dot(n1, qkv[s, i], preferred_element_type=F32).astype(BF16)], axis=0
+                )
+                for i in range(3)
+            )
             q = q * jnp.asarray(HD ** (-0.5), BF16)
-            k = jnp.dot(n1, qkv[s, 1], preferred_element_type=F32).astype(BF16)
-            v = jnp.dot(n1, qkv[s, 2], preferred_element_type=F32).astype(BF16)
             tail = jnp.zeros((KEYS - tokens, width), BF16)
             k = jnp.concatenate([k, tail], axis=0)
             values.append(jnp.concatenate([v, tail], axis=0))
@@ -515,6 +521,11 @@
     mask_copy, qkv_copy, proj_copy, up_copy, down_copy, fold_copy = copies
     for copy in (mask_copy, qkv_copy, proj_copy):
         copy.wait()
+    n_own = layer_norm(own[...].reshape(windows * half, features).astype(F32)).astype(BF16)
+    for s in range(cores):
+        for i in range(3):
+            one = jnp.dot(n_own, qkv[s, i], preferred_element_type=F32).astype(BF16)
+            ready[s, i] = one.reshape(windows, half, width)
     arrive(turn(0))
     run("a" * ORDER.count("a"), a=attend(turn(0)))
     for copy in (up_copy, down_copy, fold_copy):
@@ -607,6 +618,7 @@
             vmem((geo.tokens, cores * units), BF16),
             vmem((geo.levels - 1, cores * geo.heads * LEVEL_SLOTS, BLOCK), F32),
             vmem((geo.levels - 1, cores * geo.heads * geo.pixels, BLOCK), F32),
+            vmem((cores, 3, windows, geo.half, width), BF16),
             vmem((2 * geo.pixels, features), BF16),
             vmem((windows, geo.tokens, features), F32),
             vmem((geo.pixels, BLOCK), F32),
@@ -622,9 +634,9 @@
             dma((geo.bands, 2)),
         ],
         compiler_params=pltpu.CompilerParams(
-            collective_id=0, has_side_effects=True, vmem_limit_bytes=60 * 2**20
+            collective_id=0, has_side_effects=True, vmem_limit_bytes=30 * 2**20
         ),
-    )(*args, *tables)
+    )(*[pltpu.with_memory_space_constraint(one, pltpu.HBM) for one in (*args, *tables)])
 
 
 def assemble_kernel(isobars, run, got_ref, out_ref):

time: 37.9 us -> 34.6 us (0.913)
  Pallas kernels: 36.7 us -> 34.4 us
  local copies, waits for them, and re-layouts: 1.03 us -> 0 us
    pallas_call x1, Pallas kernels: 34.7 us -> 32.4 us  [forecast(): pl.pallas_call(functools.partial(main_kernel, geo), out_shape=jax.ShapeDt...]
    unnamed x2 -> x0, local copies, waits for them, and re-layouts: 1.03 us -> none
where the time goes in v3:
time: 34.6 us; the launch traced here: 34.4 us
  Pallas kernels  34.4 us (99%)
    pallas_call x1, Pallas kernels, forecast(): pl.pallas_call(functools.partial(main_kernel, geo), out_shape=jax.ShapeDt...  32.4 us
    pallas_call x1, Pallas kernels, assemble(): pl.pallas_call(functools.partial(assemble_kernel, isobars, run), out_shap...  1.97 us

profile of v3, /device:TPU:0, one launch (start us, length us, event | category | flops | bytes accessed | tf_op | source)
XLA Modules:
  0.0 34.4 jit_solution(9968533054851083724)
XLA Ops:
  0.0 32.4 %shard_map.154.got_ref = bf16[8,2,128,128]{3,2,1,0:T(8,128)(2,1)S(1)} custom-call(bf16[12,3,48,512]{3,2,1,0:T(8,128)(2,1)} %bitcast.3, s32[12,48]{1,0:T(8,128)} %bitcast.5, bf16[3,512,256]{2,1,0:T(8,128)(2,1)} %wqkv_ref.1, bf16[256,512]{1,0:T(8,128)(2,1)} %wproj_ref.1, bf16[512,1024]{1,0:T(8,128)(2,1)} %wup_ref.1, bf16[1024,512]{1,0:T(8,128)(2,1)} %wdown_ref.1, ...), custom_call_target="tpu_custom_call" | custom-call | tf_op jit(solution)/shard_map/pallas_call | solution.py:599
  32.5 2.0 %shard_map.155 = f32[2,13,24,384]{3,2,1,0:T(8,128)} custom-call(bf16[8,2,128,128]{3,2,1,0:T(8,128)(2,1)S(1)} %shard_map.154.got_ref), custom_call_target="tpu_custom_call" | custom-call | tf_op jit(solution)/shard_map/pallas_call | solution.py:692

commit v4 on v3

--- a/solution.py
+++ b/solution.py
@@ -28,6 +28,10 @@
     center = values - jnp.mean(values, axis=-1, keepdims=True)
     spread = jnp.mean(center * center, axis=-1, keepdims=True)
     return center * lax.rsqrt(spread + EPSILON)
+
+
+def lane_bases(bands, run):
+    return [(s * run + bands * run - run // 2) % (bands * run) for s in range(bands)]
 
 
 class Geometry:
@@ -47,7 +51,16 @@
         self.isobars = level_query.shape[0]
         self.slots = self.isobars + self.isobars % 2
         self.pixels = decode_matrix.shape[1]
-        self.scatter = bands * WIN_LAT == self.rows and (bands * self.cols * SQUARE_SPAN) % BLOCK == 0
+        self.run = self.cols * SQUARE_SPAN
+        self.extra = WIN_LAT // 2 * self.run - BLOCK
+        self.bases = lane_bases(bands, self.run)
+        covered = [(base + lane) % BLOCK for base in self.bases for lane in range(self.extra)]
+        self.scatter = (
+            bands * WIN_LAT == self.rows
+            and (bands * self.run) % BLOCK == 0
+            and self.extra * (self.slots // 2) <= BLOCK
+            and sorted(covered) == list(range(BLOCK))
+        )
 
     def place(self, half, level, r, c):
         return half * self.half + level * self.half_patches + r * self.half_cols + c
@@ -483,7 +496,8 @@
 
     def paint(w):
         low = pixels // cores
-        lane = lax.broadcasted_iota(jnp.int32, (2 * row_size, BLOCK), 1)
+        lane = lax.broadcasted_iota(jnp.int32, (2 * row_size, BLOCK), 1) - lane_base
+        lane = jnp.where(lane < 0, lane + BLOCK, lane)
         for core in range(cores):
             top = core * low
             for first_level in range(0, geo.isobars, 5):
@@ -521,6 +535,12 @@
     mask_copy, qkv_copy, proj_copy, up_copy, down_copy, fold_copy = copies
     for copy in (mask_copy, qkv_copy, proj_copy):
         copy.wait()
+    lane_base = lax.rem(grid * geo.run + bands * geo.run - geo.run // 2, BLOCK) if geo.scatter else 0
+    if geo.scatter:
+        for b in range(SQUARE_SPAN):
+            for part in range(4):
+                lanes = slice(part * BLOCK, (part + 1) * BLOCK)
+                pick[b, :, lanes] = pltpu.roll(pick[b, :, lanes].astype(F32), lane_base, 1).astype(BF16)
     n_own = layer_norm(own[...].reshape(windows * half, features).astype(F32)).astype(BF16)
     for s in range(cores):
         for i in range(3):
@@ -639,59 +659,86 @@
     )(*[pltpu.with_memory_space_constraint(one, pltpu.HBM) for one in (*args, *tables)])
 
 
-def assemble_kernel(isobars, run, got_ref, out_ref):
+def assemble_kernel(isobars, run, got_ref, out_ref, out, sems):
     bands = got_ref.shape[0]
     half_lat = WIN_LAT // 2
     groups = (isobars + 1) // 2
-    rows = groups * 16
-    whole_run = out_ref.shape[-1]
-    tiles = whole_run // BLOCK
+    tiles = out.shape[-1] // BLOCK
     extra = half_lat * run - BLOCK
-    lane = lax.broadcasted_iota(jnp.int32, (rows, BLOCK), 1)
-
-    @pl.loop(0, 2)
-    def _(ih):
-        for r in range(half_lat):
-            out = [jnp.zeros((rows, BLOCK), F32) for _ in range(tiles)]
-            for s in range(bands):
-                base = (s * run + whole_run - run // 2) % whole_run
-                piece = got_ref[s, ih].astype(F32)
-                whole = min(run, BLOCK - r * run)
-                parts = [(pltpu.roll(piece[:rows], (base - r * run) % BLOCK, 1), base, base + whole)]
-                if whole < run:
-                    rest = piece[rows:]
-                    moved = [
-                        pltpu.roll(rest, (base + whole - extra * k) % BLOCK, 1) for k in range(groups)
+    bases = lane_bases(bands, run)
+    lane = lax.broadcasted_iota(jnp.int32, (1, BLOCK), 1)
+    sublane = lax.broadcasted_iota(jnp.int32, (1, 8, BLOCK), 1)
+
+    def around(start, length):
+        start = start % BLOCK
+        if start + length <= BLOCK:
+            return jnp.logical_and(lane >= start, lane < start + length)
+        return jnp.logical_or(lane >= start, lane < start + length - BLOCK)
+
+    def put(merged, value, start, length):
+        while length > 0:
+            start = start % (tiles * BLOCK)
+            tile, part = start // BLOCK, min(length, BLOCK - start % BLOCK)
+            old = merged[tile]
+            merged[tile] = value if old is None else jnp.where(around(start, part), value, old)
+            start, length = start + part, length - part
+
+    copies = []
+    middle = (groups + 1) // 2
+    for first, last in ((0, middle), (middle, groups)):
+        low, high = 2 * first, min(2 * last, isobars)
+        found = {}
+        for ih in range(2):
+            pieces = [got_ref[s, ih, 16 * first : 16 * last, :].astype(F32) for s in range(bands)]
+            rests = [got_ref[s, ih, 16 * groups : 16 * groups + 16, :].astype(F32) for s in range(bands)]
+            left = []
+            for k in range(first, last):
+                one = rests[0]
+                for s in range(1, bands):
+                    one = jnp.where(around(bases[s] + extra * k, extra), rests[s], one)
+                left.append(pltpu.roll(one, (-extra * k) % BLOCK, 1) if k > 0 else one)
+            left = jnp.concatenate(left, axis=0)
+            for r in range(half_lat):
+                merged = [None] * tiles
+                for s in range(bands):
+                    put(merged, pieces[s], bases[s] + run * r, min(run, BLOCK - run * r))
+                if run * (r + 1) > BLOCK:
+                    for s in range(bands):
+                        put(merged, left, bases[s] + BLOCK, run * (r + 1) - BLOCK)
+                if r > 0:
+                    merged = [pltpu.roll(one, BLOCK - run * r, 1) for one in merged]
+                    merged = [
+                        jnp.where(lane < BLOCK - run * r, merged[t], merged[(t + 1) % tiles])
+                        for t in range(tiles)
                     ]
-                    parts.append((jnp.concatenate(moved, axis=0), base + whole, base + run))
-                for value, low, high in parts:
-                    spans = [(low, min(high, whole_run)), (max(low, whole_run) - whole_run, high - whole_run)]
-                    for low, high in spans:
-                        if high <= low:
-                            continue
-                        for t in range(low // BLOCK, (high - 1) // BLOCK + 1):
-                            at = lane + t * BLOCK
-                            out[t] = jnp.where(jnp.logical_and(at >= low, at < high), value, out[t])
+                found[(1 - ih) * half_lat + r] = merged
+        for top in range(0, 2 * half_lat, 2):
             for t in range(tiles):
-                value = out[t].reshape(2 * groups, 8, BLOCK)[:isobars]
-                for flag in range(2):
-                    top = ((half_lat if flag == 0 else 0) + r) * SQUARE_SPAN
-
-                    @pl.when(ih == flag)
-                    def _():
-                        for v in range(2):
-                            out_ref[v, :, top : top + SQUARE_SPAN, t * BLOCK : (t + 1) * BLOCK] = value[
-                                :, v * SQUARE_SPAN : (v + 1) * SQUARE_SPAN
-                            ]
-
-
-def assemble(got, columns, isobars):
-    bands = got.shape[0]
-    run = columns * SQUARE_SPAN
-    shape = (TARGET_QUANTITY // 2, isobars, WIN_LAT * SQUARE_SPAN, bands * run)
+                upper = found[top][t].reshape(-1, 8, BLOCK)
+                lower = found[top + 1][t].reshape(-1, 8, BLOCK)
+                some = (
+                    jnp.where(sublane < 4, upper, pltpu.roll(lower, 4, 1)),
+                    jnp.where(sublane < 4, pltpu.roll(upper, 4, 1), lower),
+                )
+                for v in range(2):
+                    out[v, low:high, 4 * top : 4 * top + 8, t * BLOCK : (t + 1) * BLOCK] = some[v][: high - low]
+        for v in range(2):
+            copy = pltpu.make_async_copy(
+                out.at[v, low:high], out_ref.at[v, low:high], sems.at[len(copies)]
+            )
+            copy.start()
+            copies.append(copy)
+    for copy in copies:
+        copy.wait()
+
+
+def assemble(got, geo):
+    shape = (TARGET_QUANTITY // geo.cores, geo.isobars, WIN_LAT * SQUARE_SPAN, geo.bands * geo.run)
     return pl.pallas_call(
-        functools.partial(assemble_kernel, isobars, run),
+        functools.partial(assemble_kernel, geo.isobars, geo.run),
         out_shape=jax.ShapeDtypeStruct(shape, F32),
+        out_specs=pl.BlockSpec(memory_space=pltpu.HBM),
+        scratch_shapes=[pltpu.VMEM(shape, F32), pltpu.SemaphoreType.DMA((4,))],
         compiler_params=pltpu.CompilerParams(vmem_limit_bytes=40 * 2**20),
     )(got)
 
@@ -748,7 +795,7 @@
         decode_matrix.T,
     )
     if geo.scatter:
-        return assemble(pieces, geo.cols, geo.isobars)
+        return assemble(pieces, geo)
     return exchange(pieces, geo)
 
 

time: 34.6 us -> 33.8 us (0.977)
  Pallas kernels: 34.4 us -> 33.7 us
    pallas_call x1, Pallas kernels: 1.97 us -> 1.25 us  [assemble(): pl.pallas_call(functools.partial(assemble_kernel, geo.isobars, geo.run),...]
where the time goes in v4:
time: 33.8 us; the launch traced here: 33.7 us
  Pallas kernels  33.7 us (100%)
    pallas_call x1, Pallas kernels, forecast(): pl.pallas_call(functools.partial(main_kernel, geo), out_shape=jax.ShapeDt...  32.4 us
    pallas_call x1, Pallas kernels, assemble(): pl.pallas_call(functools.partial(assemble_kernel, geo.isobars, geo.run),...  1.25 us

profile of v4, /device:TPU:0, one launch (start us, length us, event | category | flops | bytes accessed | tf_op | source)
XLA Modules:
  0.0 33.7 jit_solution(821083358433416374)
XLA Ops:
  0.0 32.4 %shard_map.154.got_ref = bf16[8,2,128,128]{3,2,1,0:T(8,128)(2,1)S(1)} custom-call(bf16[12,3,48,512]{3,2,1,0:T(8,128)(2,1)} %bitcast.3, s32[12,48]{1,0:T(8,128)} %bitcast.5, bf16[3,512,256]{2,1,0:T(8,128)(2,1)} %wqkv_ref.1, bf16[256,512]{1,0:T(8,128)(2,1)} %wproj_ref.1, bf16[512,1024]{1,0:T(8,128)(2,1)} %wup_ref.1, bf16[1024,512]{1,0:T(8,128)(2,1)} %wdown_ref.1, ...), custom_call_target="tpu_custom_call" | custom-call | tf_op jit(solution)/shard_map/pallas_call | solution.py:619
  32.5 1.2 %shard_map.155 = f32[2,13,24,384]{3,2,1,0:T(8,128)} custom-call(bf16[8,2,128,128]{3,2,1,0:T(8,128)(2,1)S(1)} %shard_map.154.got_ref), custom_call_target="tpu_custom_call" | custom-call | tf_op jit(solution)/shard_map/pallas_call | solution.py:737

commit v5 on v4

--- a/solution.py
+++ b/solution.py
@@ -17,7 +17,7 @@
 KEYS = 256
 CHUNK = 256
 LEVEL_SLOTS = 16
-ORDER = "abaabbbbaaabbbbabaabbbb"
+ORDER = "aabaabbbbaabbbbabababbb"
 MESH = pl.DeviceIdType.MESH
 NT = (((1,), (1,)), ((), ()))
 F32 = jnp.float32
@@ -71,15 +71,6 @@
                 for r in range(WIN_LAT):
                     for c in range(self.half_cols):
                         yield half, level, r, c
-
-    def gather_table(self):
-        table = np.zeros((self.windows, self.half, self.half_cols * self.levels * self.taken), np.float32)
-        for w in range(self.windows):
-            for half, level, r, c in self.each():
-                if half == 0:
-                    source = (c * self.levels + level) * self.taken + WIN_LAT * w + WIN_LAT // 2 + r
-                    table[w, self.place(0, level, r, c), source] = 1.0
-        return table.reshape(self.windows * self.half, -1)
 
     def order_table(self):
         table = np.zeros((self.levels * BLOCK, self.tokens), np.float32)
@@ -181,7 +172,6 @@
     wkv_ref,
     wo_ref,
     dm_ref,
-    gather_ref,
     order_ref,
     position_ref,
     perm_ref,
@@ -198,7 +188,6 @@
     wkv,
     wo,
     dm,
-    gather,
     order,
     position,
     perm,
@@ -265,13 +254,12 @@
         loads.append(copy)
         return copy
 
-    gather_load = load(gather_ref, gather)
     tiles = geo.rows // 8
     first_tile = var * (geo.row_count // 8)
     slabs = []
-    for s in range(geo.taken // 8):
-        tile = lax.rem(first_tile + s, tiles)
-        for h in (0, 1):
+    for h in (1, 0):
+        for s in range(geo.taken // 8):
+            tile = lax.rem(first_tile + s, tiles)
             some = slice(h * geo.half_cols, (h + 1) * geo.half_cols)
             slabs.append(
                 load(
@@ -299,13 +287,20 @@
 
     depth = geo.half_cols * levels * geo.taken
 
+    at = lax.broadcasted_iota(jnp.int32, (half, depth), 0)
+    level = sum(jnp.where(at >= geo.half_patches * n, 1, 0) for n in range(1, levels))
+    at = at - geo.half_patches * level
+    row = sum(jnp.where(at >= geo.half_cols * n, 1, 0) for n in range(1, WIN_LAT + 1))
+    wanted = ((at - geo.half_cols * row) * levels + level) * geo.taken + row + WIN_LAT // 2
+    wanted = jnp.where(row < WIN_LAT, wanted, depth * 2)
+    wanted = lax.broadcasted_iota(jnp.int32, (half, depth), 1) - wanted
+
     def collect(h, w, target):
         slab = raw[h * geo.half_cols : (h + 1) * geo.half_cols].reshape(depth, features)
-        picked = gather[pl.ds(pl.multiple_of(w * half, 16), half), :]
+        picked = (wanted == WIN_LAT * w).astype(F32).astype(BF16)
         target[w] = jnp.dot(picked, slab, preferred_element_type=F32).astype(BF16)
 
-    gather_load.wait()
-    for copy in slabs[1::2]:
+    for copy in slabs[: len(slabs) // 2]:
         copy.wait()
     collect(1, turn(0, east_grid), first)
     pl.semaphore_wait(barrier, greeted)
@@ -330,7 +325,7 @@
 
     for step in range(1, windows):
         collect(1, turn(step, east_grid), first)
-    for copy in slabs[0::2]:
+    for copy in slabs[len(slabs) // 2 :]:
         copy.wait()
     for step in range(windows):
         collect(0, turn(step), own)
@@ -601,7 +596,6 @@
 
 def forecast(geo, *args):
     tables = (
-        jnp.asarray(geo.gather_table(), BF16),
         jnp.asarray(geo.order_table(), BF16),
         jnp.asarray(geo.position_table(), jnp.int32),
         jnp.asarray(geo.pixel_table(), BF16),

time: 33.8 us -> 33.3 us (0.985)
  Pallas kernels: 33.7 us -> 33.2 us
    pallas_call x1, Pallas kernels: 32.4 us -> 31.9 us  [forecast(): pl.pallas_call(functools.partial(main_kernel, geo), out_shape=jax.ShapeDt...]
where the time goes in v5:
time: 33.3 us; the launch traced here: 33.2 us
  Pallas kernels  33.2 us (100%)
    pallas_call x1, Pallas kernels, forecast(): pl.pallas_call(functools.partial(main_kernel, geo), out_shape=jax.ShapeDt...  31.9 us
    pallas_call x1, Pallas kernels, assemble(): pl.pallas_call(functools.partial(assemble_kernel, geo.isobars, geo.run),...  1.25 us

profile of v5, /device:TPU:0, one launch (start us, length us, event | category | flops | bytes accessed | tf_op | source)
XLA Modules:
  0.0 33.2 jit_solution(16938322102034365761)
XLA Ops:
  0.0 31.9 %shard_map.145.got_ref = bf16[8,2,128,128]{3,2,1,0:T(8,128)(2,1)S(1)} custom-call(bf16[12,3,48,512]{3,2,1,0:T(8,128)(2,1)} %bitcast.3, s32[12,48]{1,0:T(8,128)} %bitcast.5, bf16[3,512,256]{2,1,0:T(8,128)(2,1)} %wqkv_ref.1, bf16[256,512]{1,0:T(8,128)(2,1)} %wproj_ref.1, bf16[512,1024]{1,0:T(8,128)(2,1)} %wup_ref.1, bf16[1024,512]{1,0:T(8,128)(2,1)} %wdown_ref.1, ...), custom_call_target="tpu_custom_call" | custom-call | tf_op jit(solution)/shard_map/pallas_call | solution.py:613
  31.9 1.2 %shard_map.146 = f32[2,13,24,384]{3,2,1,0:T(8,128)} custom-call(bf16[8,2,128,128]{3,2,1,0:T(8,128)(2,1)S(1)} %shard_map.145.got_ref), custom_call_target="tpu_custom_call" | custom-call | tf_op jit(solution)/shard_map/pallas_call | solution.py:731

commit v6 on v5

--- a/solution.py
+++ b/solution.py
@@ -495,19 +495,18 @@
         lane = jnp.where(lane < 0, lane + BLOCK, lane)
         for core in range(cores):
             top = core * low
-            for first_level in range(0, geo.isobars, 5):
-                some = range(first_level, min(first_level + 5, geo.isobars))
-                totals = [base_pix[top : top + low, :] for _ in some]
+            for part in range(top, top + low, 8):
+                totals = [base_pix[part : part + 8, :]] * geo.isobars
                 for s in range(cores):
                     for h in range(heads):
                         for j in range(levels - 1):
-                            at = (s * heads + h) * pixels + top
-                            value = du[j, at : at + low, :]
-                            for n, level in enumerate(some):
+                            at = (s * heads + h) * pixels + part
+                            value = du[j, at : at + 8, :]
+                            for level in range(geo.isobars):
                                 row = s * count + level * heads + h
-                                totals[n] = totals[n] + dw[j, row : row + 1, :] * value
-                for n, level in enumerate(some):
-                    pix[level, top : top + low, :] = totals[n]
+                                totals[level] = totals[level] + dw[j, row : row + 1, :] * value
+                for level in range(geo.isobars):
+                    pix[level, part : part + 8, :] = totals[level]
             total = jnp.zeros((rows, 4 * BLOCK), F32)
             for b in range(SQUARE_SPAN):
                 at = top + b * row_size

time: 33.3 us -> 32.7 us (0.982)
  Pallas kernels: 33.2 us -> 32.5 us
    pallas_call x1, Pallas kernels: 31.9 us -> 31.3 us  [forecast(): pl.pallas_call(functools.partial(main_kernel, geo), out_shape=jax.ShapeDt...]
where the time goes in v6:
time: 32.7 us; the launch traced here: 32.5 us
  Pallas kernels  32.5 us (99%)
    pallas_call x1, Pallas kernels, forecast(): pl.pallas_call(functools.partial(main_kernel, geo), out_shape=jax.ShapeDt...  31.3 us
    pallas_call x1, Pallas kernels, assemble(): pl.pallas_call(functools.partial(assemble_kernel, geo.isobars, geo.run),...  1.25 us

profile of v6, /device:TPU:0, one launch (start us, length us, event | category | flops | bytes accessed | tf_op | source)
XLA Modules:
  0.0 32.5 jit_solution(2666432064211156215)
XLA Ops:
  0.0 31.3 %shard_map.145.got_ref = bf16[8,2,128,128]{3,2,1,0:T(8,128)(2,1)S(1)} custom-call(bf16[12,3,48,512]{3,2,1,0:T(8,128)(2,1)} %bitcast.3, s32[12,48]{1,0:T(8,128)} %bitcast.5, bf16[3,512,256]{2,1,0:T(8,128)(2,1)} %wqkv_ref.1, bf16[256,512]{1,0:T(8,128)(2,1)} %wproj_ref.1, bf16[512,1024]{1,0:T(8,128)(2,1)} %wup_ref.1, bf16[1024,512]{1,0:T(8,128)(2,1)} %wdown_ref.1, ...), custom_call_target="tpu_custom_call" | custom-call | tf_op jit(solution)/shard_map/pallas_call | solution.py:612
  31.3 1.2 %shard_map.146 = f32[2,13,24,384]{3,2,1,0:T(8,128)} custom-call(bf16[8,2,128,128]{3,2,1,0:T(8,128)(2,1)S(1)} %shard_map.145.got_ref), custom_call_target="tpu_custom_call" | custom-call | tf_op jit(solution)/shard_map/pallas_call | solution.py:730

commit v7 on v6

--- a/solution.py
+++ b/solution.py
@@ -325,11 +325,12 @@
 
     for step in range(1, windows):
         collect(1, turn(step, east_grid), first)
+    pass_on(1)
     for copy in slabs[len(slabs) // 2 :]:
         copy.wait()
     for step in range(windows):
         collect(0, turn(step), own)
-    for step in range(1, windows):
+    for step in range(2, windows):
         pass_on(step)
     for copy in fold_loads:
         copy.wait()

time: 32.7 us -> 32.7 us (level)
  no operation moved by 1% of the time
where the time goes in v7:
time: 32.7 us; the launch traced here: 32.6 us
  Pallas kernels  32.5 us (99%)
    pallas_call x1, Pallas kernels, forecast(): pl.pallas_call(functools.partial(main_kernel, geo), out_shape=jax.ShapeDt...  31.3 us
    pallas_call x1, Pallas kernels, assemble(): pl.pallas_call(functools.partial(assemble_kernel, geo.isobars, geo.run),...  1.25 us

profile of v7, /device:TPU:0, one launch (start us, length us, event | category | flops | bytes accessed | tf_op | source)
XLA Modules:
  0.0 32.6 jit_solution(15781446837064644831)
XLA Ops:
  0.0 31.3 %shard_map.145.got_ref = bf16[8,2,128,128]{3,2,1,0:T(8,128)(2,1)S(1)} custom-call(bf16[12,3,48,512]{3,2,1,0:T(8,128)(2,1)} %bitcast.3, s32[12,48]{1,0:T(8,128)} %bitcast.5, bf16[3,512,256]{2,1,0:T(8,128)(2,1)} %wqkv_ref.1, bf16[256,512]{1,0:T(8,128)(2,1)} %wproj_ref.1, bf16[512,1024]{1,0:T(8,128)(2,1)} %wup_ref.1, bf16[1024,512]{1,0:T(8,128)(2,1)} %wdown_ref.1, ...), custom_call_target="tpu_custom_call" | custom-call | tf_op jit(solution)/shard_map/pallas_call | solution.py:613
  31.3 1.2 %shard_map.146 = f32[2,13,24,384]{3,2,1,0:T(8,128)} custom-call(bf16[8,2,128,128]{3,2,1,0:T(8,128)(2,1)S(1)} %shard_map.145.got_ref), custom_call_target="tpu_custom_call" | custom-call | tf_op jit(solution)/shard_map/pallas_call | solution.py:731
